TPU v7x, 512 devices: a whole 4x4x16 slice. The times are simulated.
512 devices in a mesh: row: 16 (over x_hi, y, core), col: 32 (over z, x_lo).
Axes of the slice: x: 4 (x_hi: 2, x_lo: 2; x = x_hi * 2 + x_lo), y: 4, z: 16, core: 2. Of those that a mesh axis runs over, the one named last changes fastest.
Arguments:
- tokens: bfloat16 [256, 16384], P('row', 'col'), may hold values from -6 to 6
- gate_weight: bfloat16 [16384, 26624], P('col', 'row'), may hold values from -0.046875 to 0.046875
- up_weight: bfloat16 [16384, 26624], P('col', 'row'), may hold values from -0.046875 to 0.046875
Outputs:
- hidden: bfloat16 [256, 26624], P(None, 'row')
All inputs are finite; a program needn't handle non-finite values.
Results may differ from a plain program's by a relative error of at most 0.001.
Values may be sent and summed in bfloat16 or wider, within the bound.
No kernel may reach another device: no remote copies, remote signals or barrier semaphores. Data moves between devices by JAX's collectives and lax.ppermute only.
A program may use at most 64 MiB of HBM per device.

v0:
```python
import jax
import jax.numpy as jnp
from jax import lax
from jax.sharding import Mesh
from jax.sharding import PartitionSpec as P

COL = ("col_0", "col_1")


def laid_out(pieces, dim):
    pieces = jnp.moveaxis(pieces, 0, dim)
    lengths = pieces.shape
    return pieces.reshape(*lengths[:dim], lengths[dim] * lengths[dim + 1], *lengths[dim + 2 :])


def copy_for_each(value, axis):
    devices = lax.axis_size(axis)
    return lax.all_to_all(
        jnp.broadcast_to(value[None], (devices, *value.shape)), axis, 0, 0, tiled=True
    )


def gather_directly(value, axis, dim):
    return laid_out(copy_for_each(value, axis), dim)


def summed_rows(value, axes, dim):
    if not axes:
        return value
    nearer = lax.psum_scatter(value, axes[0], scatter_dimension=dim, tiled=True)
    return summed_rows(nearer, axes[1:], dim)


def gathered_by_axis(value, axes, dim):
    if not axes:
        return value
    nearer = lax.all_gather(value, axes[-1], axis=dim, tiled=True)
    return gathered_by_axis(nearer, axes[:-1], dim)


def local(tokens, gate_weight, up_weight):
    columns = gate_weight.shape[1]
    block_rows = gather_directly(tokens, "row", 0)
    gate_term = jnp.dot(block_rows, gate_weight, preferred_element_type=jnp.float32)
    up_term = jnp.dot(block_rows, up_weight, preferred_element_type=jnp.float32)
    partial_value = jnp.concatenate([gate_term, up_term], axis=1)
    shared = summed_rows(partial_value, COL, 0)
    gated = (jax.nn.silu(shared[:, :columns]) * shared[:, columns:]).astype(jnp.bfloat16)
    hidden = gathered_by_axis(gated, COL, 0)
    return hidden


def solution(mesh):
    split = Mesh(mesh.devices.reshape(mesh.shape["row"], 16, 2), ("row", "col_0", "col_1"))
    return jax.shard_map(
        local,
        mesh=split,
        in_specs=(P("row", COL), P(COL, "row"), P(COL, "row")),
        out_specs=P(None, "row"),
        check_vma=False,
    )
```

profile of v0, /device:TPU:16, one launch (start us, length us, event | category | flops | bytes accessed | tf_op | source)
XLA Modules:
  0.0 176.7 jit_solution(9003333131844445725)
XLA Ops:
  6.5 0.0 copy-start
  6.5 0.0 reduce-scatter.3.cloned.1.call-start
  6.5 0.9 broadcast_in_dim.2
  7.4 14.5 %all_to_all.5 = bf16[16,16,512]{2,1,0:T(8,128)(2,1)S(1)} all-to-all(bf16[16,16,512]{2,1,0:T(8,128)(2,1)S(1)} %broadcast_in_dim.2), channel_id=1, replica_groups=mesh['row'=16,'col_0'=16,'col_1'=2] {'row'}, dimensions={0} | all-to-all | bytes 524288 | tf_op jit(solution)/shard_map/all_to_all | solution.py:18
  21.9 0.0 copy-done
  21.9 0.0 copy-start.1
  21.9 0.6 fusion.2
  22.5 0.8 copy-done.1
  23.3 0.6 fusion.1
  24.0 2.0 %pad_maximum_fusion = f32[256,3328]{1,0:T(8,128)} fusion(f32[256,1664]{1,0:T(8,128)S(1)} %fusion.2, f32[256,1664]{1,0:T(8,128)S(1)} %fusion.1), kind=kLoop, calls=%fused_computation | loop fusion | flops 851968 | bytes 6815744 | tf_op jit(solution)/shard_map/concatenate | solution.py:46
  25.9 0.0 reduce-scatter.3.cloned.1.call-update
  26.0 0.0 reduce-scatter.5.cloned.1.call-start
  26.0 80.3 %reduce-scatter.3.cloned.1.call-done = f32[16,3328]{1,0:T(8,128)} async-done(((f32[256,3328]{1,0:T(8,128)}), f32[16,3328]{1,0:T(8,128)}) %reduce-scatter.3.cloned.1.call-update) | async-done | bytes 213008 | tf_op jit(solution)/shard_map/reduce_scatter | solution.py:30
  106.3 0.0 reduce-scatter.5.cloned.1.call-update
  106.3 21.6 %reduce-scatter.5.cloned.1.call-done = f32[8,3328]{1,0:T(8,128)} async-done(((f32[16,3328]{1,0:T(8,128)}), f32[8,3328]{1,0:T(8,128)}) %reduce-scatter.5.cloned.1.call-update) | async-done | bytes 106512 | tf_op jit(solution)/shard_map/reduce_scatter | solution.py:30
  127.9 0.9 fusion
  128.8 4.5 %all_gather.6 = bf16[16,1664]{1,0:T(8,128)(2,1)S(1)} all-gather(bf16[8,1664]{1,0:T(8,128)(2,1)S(1)} %fusion), channel_id=1, replica_groups=mesh['row'=16,'col_0'=16,'col_1'=2] {'col_1'}, dimensions={0}, use_global_device_ids=true | all-gather | bytes 79872 | tf_op jit(solution)/shard_map/all_gather | solution.py:37
  133.3 35.7 %all_gather.7 = bf16[256,1664]{1,0:T(8,128)(2,1)S(1)} all-gather(bf16[16,1664]{1,0:T(8,128)(2,1)S(1)} %all_gather.6), channel_id=1, replica_groups=mesh['row'=16,'col_0'=16,'col_1'=2] {'col_0'}, dimensions={0}, use_global_device_ids=true | all-gather | bytes 905216 | tf_op jit(solution)/shard_map/all_gather | solution.py:37
  169.0 0.9 copy.5
Async XLA Ops:
  6.5 15.3 %copy-start = (bf16[512,1664]{1,0:T(8,128)(2,1)S(1)}, bf16[512,1664]{1,0:T(8,128)(2,1)}, u32[]{:S(2)}) copy-start(bf16[512,1664]{1,0:T(8,128)(2,1)} %param.5) | copy-start | bytes 5111812
  6.5 99.8 %reduce-scatter.3.cloned.1.call-start = ((), (), s32[]{:S(2)}) async-start(), calls=%async_computation.3 | async-start | bytes 3620864 | tf_op jit(solution)/shard_map/reduce_scatter | solution.py:30
  21.9 1.5 copy-start.1
  26.0 102.0 %reduce-scatter.5.cloned.1.call-start = ((), (), s32[]{:S(2)}) async-start(), calls=%async_computation.4 | async-start | bytes 319488 | tf_op jit(solution)/shard_map/reduce_scatter | solution.py:30
Sparse Core Ops, SparseCore 0:
  26.1 80.1 reduce-scatter.2
  109.1 18.8 reduce-scatter.4
where the time goes:
time: 177 us
  waiting for transfers between devices  102 us (58%)
  blocking collectives  54.7 us (31%)
  between operations  13.4 us (8%)
  other arithmetic  2.81 us (2%)
  local copies, waits for them, and re-layouts  2.57 us (1%)
    reduce_scatter x2, waiting for transfers between devices, summed_rows(): nearer = lax.psum_scatter(value, axes[0], scatter_dimension=dim, tiled=True)  102 us
    all_gather x2, blocking collectives, gathered_by_axis(): nearer = lax.all_gather(value, axes[-1], axis=dim, tiled=True)  40.2 us
    all_to_all x1, blocking collectives, copy_for_each(): lax.all_to_all(jnp.broadcast_to(value[None], (devices, *value.shape)), ax...  14.5 us
  transfers between devices with their start and end apart: 2, of which 2 were waited for; matrix products, arithmetic and copies ran while one was open for 0% of the time, Pallas kernels for 0%

commit v1 on v0

v1 whole, which is shorter than its diff:
```python
import jax
import jax.numpy as jnp
from jax import lax
from jax.sharding import Mesh
from jax.sharding import PartitionSpec as P

ROW = "row"
FAR = "z_far"
NEAR = ("z_near", "x_lo")
LANES = 128
HALF_RANGE = 125.0


def copy_for_each(value, axis):
    devices = lax.axis_size(axis)
    return lax.all_to_all(
        jnp.broadcast_to(value[None], (devices, *value.shape)), axis, 0, 0, tiled=True
    )


def gathered(value, axis):
    pieces = copy_for_each(value, axis)
    return pieces.reshape(pieces.shape[0] * pieces.shape[1], *pieces.shape[2:])


def coded(rows):
    largest = jnp.max(jnp.abs(rows), axis=-1, keepdims=True)
    largest = jnp.maximum(largest * (1.0 + 2.0**-6), 1e-30).astype(jnp.bfloat16)
    scale = (2.0 * HALF_RANGE) / largest.astype(jnp.float32)
    power = jnp.exp2(jnp.abs(rows) * scale - HALF_RANGE)
    code = jnp.where(rows < 0, -power, power).astype(jnp.bfloat16)
    return jnp.concatenate(
        [code, jnp.broadcast_to(largest, (*largest.shape[:-1], LANES))], axis=-1
    )


def decoded(message):
    code = message[..., :-LANES].astype(jnp.float32)
    largest = message[..., -LANES:][..., :1].astype(jnp.float32)
    size = (jnp.log2(jnp.abs(code)) + HALF_RANGE) * (largest / (2.0 * HALF_RANGE))
    return jnp.where(code < 0, -size, size)


def summed_rows(value, axis):
    devices = lax.axis_size(axis)
    message = coded(value)
    pieces = lax.all_to_all(
        message.reshape(devices, message.shape[0] // devices, message.shape[1]), axis, 0, 0, tiled=True
    )
    return jnp.sum(decoded(pieces), axis=0)


def local(tokens, gate_weight, up_weight):
    columns = gate_weight.shape[1]
    block_rows = gathered(tokens, ROW)
    gate_term = jnp.dot(block_rows, gate_weight, preferred_element_type=jnp.float32)
    up_term = jnp.dot(block_rows, up_weight, preferred_element_type=jnp.float32)
    partial_value = jnp.concatenate([gate_term, up_term], axis=1)
    total = summed_rows(summed_rows(partial_value, NEAR), FAR)
    gated = (jax.nn.silu(total[:, :columns]) * total[:, columns:]).astype(jnp.bfloat16)
    return gathered(gathered(gated, FAR), NEAR)


def solution(mesh):
    split = Mesh(
        mesh.devices.reshape(mesh.shape["row"], 8, 2, 2), ("row", "z_far", "z_near", "x_lo")
    )
    col = ("z_far", "z_near", "x_lo")
    return jax.shard_map(
        local,
        mesh=split,
        in_specs=(P("row", col), P(col, "row"), P(col, "row")),
        out_specs=P(None, "row"),
        check_vma=False,
    )
```

time: 177 us -> 136 us (0.77)
  the two profiles are of different devices: /device:TPU:16 before, /device:TPU:72 now
where the time goes in v1:
time: 136 us
  blocking collectives  118 us (87%)
  other arithmetic  8.36 us (6%)
  local copies, waits for them, and re-layouts  7.81 us (6%)
    all_to_all x2, blocking collectives, summed_rows(): lax.all_to_all(message.reshape(devices, message.shape[0] // devices, mess...  68.1 us
    all_to_all x3, blocking collectives, copy_for_each(): lax.all_to_all(jnp.broadcast_to(value[None], (devices, *value.shape)), ax...  50.1 us
    unnamed x8, local copies, waits for them, and re-layouts  4.59 us
    abs x1, other arithmetic, coded(): power = jnp.exp2(jnp.abs(rows) * scale - HALF_RANGE)  3.02 us
    convert_element_type x2, other arithmetic, coded(): code = jnp.where(rows < 0, -power, power).astype(jnp.bfloat16)  2.89 us

profile of v1, /device:TPU:72, one launch (start us, length us, event | category | flops | bytes accessed | tf_op | source)
XLA Modules:
  0.0 135.8 jit_solution(10123134672992616512)
XLA Ops:
  0.0 0.0 copy-start
  0.0 0.9 broadcast_in_dim.12
  0.9 14.0 %all_to_all.25 = bf16[16,16,512]{2,1,0:T(8,128)(2,1)S(1)} all-to-all(bf16[16,16,512]{2,1,0:T(8,128)(2,1)S(1)} %broadcast_in_dim.12), channel_id=1, replica_groups=mesh['row'=16,'z_far'=8,'z_near'=2,'x_lo'=2] {'row'}, dimensions={0} | all-to-all | bytes 524288 | tf_op jit(solution)/shard_map/all_to_all | solution.py:16
  14.9 0.0 copy-done
  14.9 0.0 copy-start.2
  14.9 0.6 fusion.19
  15.5 0.8 copy-done.2
  16.3 0.6 fusion.18
  17.0 0.0 copy-start.1
  17.0 1.2 copy-done.1
  18.2 0.4 fusion.6
  18.5 0.1 convert_element_type.68
  18.6 2.6 %fusion.4 = bf16[4,64,3328]{2,1,0:T(8,128)(2,1)S(1)} fusion(f32[4,64,1664]{2,1,0:T(8,128)S(1)} %bitcast.21, f32[4,64,1664]{2,1,0:T(8,128)} %bitcast.22, f32[4,64]{1,0:T(4,128)S(1)} %convert_divide_fusion.1), kind=kLoop, calls=%fused_computation.8 | loop fusion | flops 7667712 | bytes 5112832 | tf_op jit(solution)/shard_map/convert_element_type | solution.py:31
  21.2 0.1 broadcast_in_dim.13
  21.3 0.1 pad_maximum_fusion.1
  21.5 26.1 %all_to_all.26 = bf16[4,64,3456]{2,1,0:T(8,128)(2,1)S(1)} all-to-all(bf16[4,64,3456]{2,1,0:T(8,128)(2,1)S(1)} %pad_maximum_fusion.1), channel_id=1, replica_groups=mesh['row'=16,'z_far'=8,'z_near'=2,'x_lo'=2] {'z_near','x_lo'}, dimensions={0} | all-to-all | bytes 3538944 | tf_op jit(solution)/shard_map/all_to_all | solution.py:47
  47.6 0.1 multiply_reduce_fusion
  47.7 1.3 fusion.5
  49.1 1.7 %copy.14 = f32[64,3328]{0,1:T(8,128)} copy(f32[64,3328]{1,0:T(8,128)S(1)} %fusion.5) | data formatting | bytes 1703936
  50.8 3.0 %fusion.17 = (f32[64,3328]{0,1:T(8,128)}, f32[64]{0:T(128)S(1)}) fusion(f32[64,3328]{0,1:T(8,128)} %copy.14), kind=kLoop, calls=%fused_computation.38 | loop fusion | flops 425920 | bytes 1704192 | tf_op jit(solution)/shard_map/abs | solution.py:30
  53.8 1.9 %copy.13 = f32[64,3328]{1,0:T(8,128)S(1)} copy(f32[64,3328]{0,1:T(8,128)} %get-tuple-element.5) | data formatting | bytes 1703936 | tf_op jit(solution)/shard_map/abs | solution.py:30
  55.7 0.1 convert_element_type.74
  55.8 0.3 fusion.11
  56.2 0.1 broadcast_in_dim.14
  56.3 41.9 %all_to_all.27 = bf16[8,8,3456]{2,1,0:T(8,128)(2,1)S(1)} all-to-all(bf16[8,8,3456]{2,1,0:T(8,128)(2,1)S(1)} %pad_maximum_fusion.2), channel_id=1, replica_groups=mesh['row'=16,'z_far'=8,'z_near'=2,'x_lo'=2] {'z_far'}, dimensions={0} | all-to-all | bytes 884736 | tf_op jit(solution)/shard_map/all_to_all | solution.py:47
  98.2 0.1 multiply_reduce_fusion.1
  98.3 0.3 fusion.12
  98.7 21.3 %all_to_all.28 = bf16[8,8,1664]{2,1,0:T(8,128)(2,1)S(1)} all-to-all(bf16[8,8,1664]{2,1,0:T(8,128)(2,1)S(1)} %broadcast_in_dim.15), channel_id=1, replica_groups=mesh['row'=16,'z_far'=8,'z_near'=2,'x_lo'=2] {'z_far'}, dimensions={0} | all-to-all | bytes 425984 | tf_op jit(solution)/shard_map/all_to_all | solution.py:16
  120.0 0.1 broadcast_in_dim.17
  120.1 14.8 %all_to_all.29 = bf16[4,64,1664]{2,1,0:T(8,128)(2,1)S(1)} all-to-all(bf16[4,64,1664]{2,1,0:T(8,128)(2,1)S(1)} %broadcast_in_dim.17), channel_id=1, replica_groups=mesh['row'=16,'z_far'=8,'z_near'=2,'x_lo'=2] {'z_near','x_lo'}, dimensions={0} | all-to-all | bytes 1703936 | tf_op jit(solution)/shard_map/all_to_all | solution.py:16
  134.9 0.9 copy.16
  (7 shorter events, 0.1 us)
Async XLA Ops:
  0.0 14.9 %copy-start = (bf16[512,1664]{1,0:T(8,128)(2,1)S(1)}, bf16[512,1664]{1,0:T(8,128)(2,1)}, u32[]{:S(2)}) copy-start(bf16[512,1664]{1,0:T(8,128)(2,1)} %param.5) | copy-start | bytes 5111812
  14.9 1.5 %copy-start.2 = (bf16[512,1664]{1,0:T(8,128)(2,1)S(1)}, bf16[512,1664]{1,0:T(8,128)(2,1)}, u32[]{:S(2)}) copy-start(bf16[512,1664]{1,0:T(8,128)(2,1)} %param.4) | copy-start | bytes 5111812
  17.0 1.2 copy-start.1

commit v2 on v1

v2 whole, which is shorter than its diff:
```python
import functools

import jax
import jax.numpy as jnp
from jax import lax
from jax.experimental import pallas as pl
from jax.experimental.pallas import tpu as pltpu
from jax.sharding import Mesh
from jax.sharding import PartitionSpec as P

ROW = "row"
FAR = "z_far"
NEAR = ("z_near", "x_lo")
COL = (FAR, *NEAR)
LANES = 128
ROWS = 8
HALF_RANGE = 125.0


def copy_for_each(value, axis):
    devices = lax.axis_size(axis)
    return lax.all_to_all(
        jnp.broadcast_to(value[None], (devices, *value.shape)), axis, 0, 0, tiled=True
    )


def gathered(value, axis):
    pieces = copy_for_each(value, axis)
    return pieces.reshape(pieces.shape[0] * pieces.shape[1], *pieces.shape[2:])


def largest_of(tiles):
    peak = functools.reduce(jnp.maximum, [jnp.abs(tile) for tile in tiles])
    peak = jnp.max(peak, axis=-1, keepdims=True)
    return jnp.maximum(peak * (1.0 + 2.0**-6), 1e-30).astype(jnp.bfloat16).astype(jnp.float32)


def coded(tile, scale):
    power = jnp.exp2(jnp.abs(tile) * scale - HALF_RANGE)
    return jnp.where(tile < 0, -power, power)


def decoded(code, unit):
    code = code.astype(jnp.float32)
    size = (jnp.log2(jnp.abs(code)) + HALF_RANGE) * unit
    return jnp.where(code < 0, -size, size)


def lanes_of(tile):
    return pl.ds(tile * LANES, LANES)


def write_rows(values, message):
    tiles = [values[:, lanes_of(t)] for t in range(values.shape[1] // LANES)]
    largest = largest_of(tiles)
    scale = (2.0 * HALF_RANGE) / largest
    for t, tile in enumerate(tiles):
        message[:, lanes_of(t)] = coded(tile, scale).astype(jnp.bfloat16)
    mark = jnp.broadcast_to(largest, (largest.shape[0], LANES))
    message[:, lanes_of(len(tiles))] = mark.astype(jnp.bfloat16)


def sum_of(message, rows, tile, units):
    return sum(decoded(message[d, rows, lanes_of(tile)], unit) for d, unit in enumerate(units))


def units_of(message, rows):
    last = message.shape[2] // LANES - 1
    return [
        message[d, rows, lanes_of(last)].astype(jnp.float32) * (0.5 / HALF_RANGE)
        for d in range(message.shape[0])
    ]


def first_body(tokens, gate_weight, up_weight, message, values, held, arrivals):
    columns = gate_weight.shape[1]
    copies = [
        pltpu.make_async_copy(weight, held.at[i], arrivals.at[i])
        for i, weight in enumerate((gate_weight, up_weight))
    ]
    for copy in copies:
        copy.start()
    for i, copy in enumerate(copies):
        copy.wait()
        values[:, i * columns : (i + 1) * columns] = jnp.dot(
            tokens[...], held[i], preferred_element_type=jnp.float32
        )
    for block in range(message.shape[0]):
        @pl.loop(0, message.shape[1], step=2 * ROWS)
        def _(start):
            start = pl.multiple_of(start, 2 * ROWS)
            write_rows(
                values.at[pl.ds(block * message.shape[1] + start, 2 * ROWS)],
                message.at[block, pl.ds(start, 2 * ROWS)],
            )


def second_body(pieces, message, values):
    @pl.loop(0, pieces.shape[1], step=2 * ROWS)
    def _(start):
        rows = pl.ds(pl.multiple_of(start, 2 * ROWS), 2 * ROWS)
        units = units_of(pieces, rows)
        for t in range(values.shape[1] // LANES):
            values[rows, lanes_of(t)] = sum_of(pieces, rows, t, units)

    @pl.loop(0, message.shape[0])
    def _(far):
        write_rows(values.at[pl.ds(pl.multiple_of(far * ROWS, ROWS), ROWS)], message.at[far])


def third_body(pieces, copies):
    rows = pl.ds(0, pieces.shape[1])
    units = units_of(pieces, rows)
    tiles = copies.shape[2] // LANES
    for t in range(tiles):
        gate, up = sum_of(pieces, rows, t, units), sum_of(pieces, rows, t + tiles, units)
        hidden = (gate / (1.0 + jnp.exp(-gate)) * up).astype(jnp.bfloat16)
        for d in range(copies.shape[0]):
            copies[d, :, lanes_of(t)] = hidden


def on_chip(body, shape, *operands, stored=(), scratch=()):
    on_chip_operands = [pltpu.with_memory_space_constraint(value, pltpu.VMEM) for value in operands]
    return pl.pallas_call(
        body,
        in_specs=[pl.BlockSpec(memory_space=pltpu.VMEM)] * len(operands)
        + [pl.BlockSpec(memory_space=pl.ANY)] * len(stored),
        out_specs=pl.BlockSpec(memory_space=pltpu.VMEM),
        out_shape=pltpu.VMEM(shape, jnp.bfloat16),
        scratch_shapes=scratch,
        compiler_params=pltpu.CompilerParams(vmem_limit_bytes=16 * 2**20),
    )(*on_chip_operands, *stored)


def local(tokens, gate_weight, up_weight):
    columns = gate_weight.shape[1]
    width = 2 * columns + LANES
    block_rows = gathered(tokens, ROW)
    count = block_rows.shape[0]
    near = lax.axis_size(NEAR)
    far = lax.axis_size(FAR)
    coded_parts = on_chip(
        first_body,
        (near, count // near, width),
        block_rows,
        stored=(gate_weight, up_weight),
        scratch=[
            pltpu.VMEM((count, 2 * columns), jnp.float32),
            pltpu.VMEM((2, *gate_weight.shape), jnp.bfloat16),
            pltpu.SemaphoreType.DMA((2,)),
        ],
    )
    near_parts = lax.all_to_all(coded_parts, NEAR, 0, 0, tiled=True)
    coded_sums = on_chip(
        second_body,
        (far, ROWS, width),
        near_parts,
        scratch=[pltpu.VMEM((count // near, 2 * columns), jnp.float32)],
    )
    far_parts = lax.all_to_all(coded_sums, FAR, 0, 0, tiled=True)
    copies = on_chip(third_body, (far, ROWS, columns), far_parts)
    hidden = lax.all_to_all(copies, FAR, 0, 0, tiled=True).reshape(count // near, columns)
    return gathered(hidden, NEAR)


def solution(mesh):
    split = Mesh(mesh.devices.reshape(mesh.shape["row"], 8, 2, 2), (ROW, *COL))
    return jax.shard_map(
        local,
        mesh=split,
        in_specs=(P(ROW, COL), P(COL, ROW), P(COL, ROW)),
        out_specs=P(None, ROW),
        check_vma=False,
    )
```

time: 136 us -> 130 us (0.956)
  other arithmetic: 8.36 us -> 0 us
  Pallas kernels: 0 us -> 7.15 us
  local copies, waits for them, and re-layouts: 7.81 us -> 4.6 us
    all_to_all x2 -> x3, blocking collectives: 68.1 us -> 89.4 us  [the longest x1 41.9 us: local(): far_parts = lax.all_to_all(coded_sums, FAR, 0, 0, tiled=True)]
    all_to_all x3 -> x2, blocking collectives: 50.1 us -> 28.8 us  [copy_for_each(): lax.all_to_all(jnp.broadcast_to(value[None], (devices, *value.shape)), ax...]
    pallas_call x0 -> x3, Pallas kernels: none -> 7.15 us  [on_chip(): pl.pallas_call(body, in_specs=[pl.BlockSpec(memory_space=pltpu.VMEM)] * l...]
    abs x1 -> x0, other arithmetic: 3.02 us -> none  [coded(): power = jnp.exp2(jnp.abs(rows) * scale - HALF_RANGE)]
    convert_element_type x5 -> x0, other arithmetic: 2.93 us -> none  [the longest x2 2.89 us: coded(): code = jnp.where(rows < 0, -power, power).astype(jnp.bfloat16)]
    abs x1 -> x0, local copies, waits for them, and re-layouts: 1.93 us -> none  [coded(): power = jnp.exp2(jnp.abs(rows) * scale - HALF_RANGE)]
    reduce_sum x2 -> x0, other arithmetic: 1.66 us -> none  [summed_rows(): return jnp.sum(decoded(pieces), axis=0)]
    unnamed x8 -> x5, local copies, waits for them, and re-layouts: 4.59 us -> 3.81 us
where the time goes in v2:
time: 130 us
  blocking collectives  118 us (91%)
  Pallas kernels  7.15 us (6%)
  local copies, waits for them, and re-layouts  4.6 us (4%)
    all_to_all x1, blocking collectives, local(): far_parts = lax.all_to_all(coded_sums, FAR, 0, 0, tiled=True)  41.9 us
    all_to_all x2, blocking collectives, copy_for_each(): lax.all_to_all(jnp.broadcast_to(value[None], (devices, *value.shape)), ax...  28.8 us
    all_to_all x1, blocking collectives, local(): near_parts = lax.all_to_all(coded_parts, NEAR, 0, 0, tiled=True)  26.1 us
    all_to_all x1, blocking collectives, local(): lax.all_to_all(copies, FAR, 0, 0, tiled=True)  21.3 us
    pallas_call x3, Pallas kernels, on_chip(): pl.pallas_call(body, in_specs=[pl.BlockSpec(memory_space=pltpu.VMEM)] * l...  7.15 us
    unnamed x5, local copies, waits for them, and re-layouts  3.81 us

profile of v2, /device:TPU:72, one launch (start us, length us, event | category | flops | bytes accessed | tf_op | source)
XLA Modules:
  0.0 130.0 jit_solution(13921077692077617223)
XLA Ops:
  0.0 0.7 broadcast_in_dim.6
  0.7 14.0 %all_to_all.25 = bf16[16,16,512]{2,1,0:T(8,128)(2,1)S(1)} all-to-all(bf16[16,16,512]{2,1,0:T(8,128)(2,1)S(1)} %broadcast_in_dim.6), channel_id=1, replica_groups=mesh['row'=16,'z_far'=8,'z_near'=2,'x_lo'=2] {'row'}, dimensions={0} | all-to-all | bytes 524288 | tf_op jit(solution)/shard_map/all_to_all | solution.py:22
  14.8 0.0 copy-start
  14.8 1.5 %copy-done = bf16[512,1664]{1,0:T(8,128)(2,1)S(1)} copy-done((bf16[512,1664]{1,0:T(8,128)(2,1)S(1)}, bf16[512,1664]{1,0:T(8,128)(2,1)}, u32[]{:S(2)}) %copy-start) | copy-done | bytes 1703960
  16.2 0.0 copy-start.1
  16.2 1.5 %copy-done.1 = bf16[512,1664]{1,0:T(8,128)(2,1)S(1)} copy-done((bf16[512,1664]{1,0:T(8,128)(2,1)S(1)}, bf16[512,1664]{1,0:T(8,128)(2,1)}, u32[]{:S(2)}) %copy-start.1) | copy-done | bytes 1703960
  17.7 4.8 %shard_map.37 = bf16[4,64,3456]{2,1,0:T(8,128)(2,1)S(1)} custom-call(bf16[256,512]{1,0:T(8,128)(2,1)S(1)} %bitcast.3, bf16[512,1664]{1,0:T(8,128)(2,1)S(1)} %copy-done, bf16[512,1664]{1,0:T(8,128)(2,1)S(1)} %copy-done.1), custom_call_target="tpu_custom_call" | custom-call | tf_op jit(solution)/shard_map/pallas_call | solution.py:124
  22.5 26.1 %all_to_all.26.pieces = bf16[4,64,3456]{2,1,0:T(8,128)(2,1)S(1)} all-to-all(bf16[4,64,3456]{2,1,0:T(8,128)(2,1)S(1)} %shard_map.37), channel_id=1, replica_groups=mesh['row'=16,'z_far'=8,'z_near'=2,'x_lo'=2] {'z_near','x_lo'}, dimensions={0} | all-to-all | bytes 3538944 | tf_op jit(solution)/shard_map/all_to_all | solution.py:153
  48.6 2.1 %shard_map.38 = bf16[8,8,3456]{2,1,0:T(8,128)(2,1)S(1)} custom-call(bf16[4,64,3456]{2,1,0:T(8,128)(2,1)S(1)} %all_to_all.26.pieces), custom_call_target="tpu_custom_call" | custom-call | tf_op jit(solution)/shard_map/pallas_call | solution.py:124
  50.7 41.9 %all_to_all.27.pieces = bf16[8,8,3456]{2,1,0:T(8,128)(2,1)S(1)} all-to-all(bf16[8,8,3456]{2,1,0:T(8,128)(2,1)S(1)} %shard_map.38), channel_id=1, replica_groups=mesh['row'=16,'z_far'=8,'z_near'=2,'x_lo'=2] {'z_far'}, dimensions={0} | all-to-all | bytes 884736 | tf_op jit(solution)/shard_map/all_to_all | solution.py:160
  92.6 0.3 shard_map.39
  92.9 21.3 %all_to_all.28 = bf16[8,8,1664]{2,1,0:T(8,128)(2,1)S(1)} all-to-all(bf16[8,8,1664]{2,1,0:T(8,128)(2,1)S(1)} %shard_map.39), channel_id=1, replica_groups=mesh['row'=16,'z_far'=8,'z_near'=2,'x_lo'=2] {'z_far'}, dimensions={0} | all-to-all | bytes 425984 | tf_op jit(solution)/shard_map/all_to_all | solution.py:162
  114.2 0.1 broadcast_in_dim.15
  114.3 14.8 %all_to_all.29 = bf16[4,64,1664]{2,1,0:T(8,128)(2,1)S(1)} all-to-all(bf16[4,64,1664]{2,1,0:T(8,128)(2,1)S(1)} %broadcast_in_dim.15), channel_id=1, replica_groups=mesh['row'=16,'z_far'=8,'z_near'=2,'x_lo'=2] {'z_near','x_lo'}, dimensions={0} | all-to-all | bytes 1703936 | tf_op jit(solution)/shard_map/all_to_all | solution.py:22
  129.1 0.9 copy.5
Async XLA Ops:
  14.8 1.5 %copy-start = (bf16[512,1664]{1,0:T(8,128)(2,1)S(1)}, bf16[512,1664]{1,0:T(8,128)(2,1)}, u32[]{:S(2)}) copy-start(bf16[512,1664]{1,0:T(8,128)(2,1)} %gate_weight.1) | copy-start | bytes 5111812
  16.2 1.5 %copy-start.1 = (bf16[512,1664]{1,0:T(8,128)(2,1)S(1)}, bf16[512,1664]{1,0:T(8,128)(2,1)}, u32[]{:S(2)}) copy-start(bf16[512,1664]{1,0:T(8,128)(2,1)} %up_weight.1) | copy-start | bytes 5111812
